TPU v7x, 128 devices: a whole 4x4x4 slice. The times are simulated.
128 devices in a mesh: row: 16 (over y, z_hi, core), col: 8 (over x, z_lo).
Axes of the slice: x: 4, y: 4, z: 4 (z_hi: 2, z_lo: 2; z = z_hi * 2 + z_lo), core: 2. Of those that a mesh axis runs over, the one named last changes fastest.
Arguments:
- homolog_embedding: bfloat16 [128, 1024, 64], P(('row', 'col')), may hold values from -6 to 6
- split_mapping_matrix: bfloat16 [64, 64], replicated, may hold values from -0.75 to 0.75
- couple_mapping_matrix: bfloat16 [1024, 128], replicated, may hold values from -1.5 to 1.5
- couple_offset_vector: bfloat16 [128], replicated, may hold values from -3 to 3
- incoming_adjoint_couple: bfloat16 [1024, 1024, 128], P('row', 'col'), may hold values from -0.29882812 to 0.29882812
Outputs:
- pair_delta_output: bfloat16 [1024, 1024, 128], P('row', 'col')
- alignment_gradient: bfloat16 [128, 1024, 64], P(('row', 'col'))
- out_weight_grad: float32 [1024, 128], replicated
All inputs are finite; a program needn't handle non-finite values.
Results may differ from a plain program's by a relative error of at most 0.015.
Values may be sent and summed in bfloat16 or wider, within the bound.
A program may use at most 64 MiB of HBM per device.

v0:
```python
import math
import jax
import jax.numpy as jnp
from jax import lax
from jax.sharding import PartitionSpec as P


def copy_for_each(array, axis):
    size = lax.axis_size(axis)
    return lax.all_to_all(
        jnp.broadcast_to(array[None], (size, *array.shape)), axis, 0, 0, tiled=True
    )


def laid_out(pieces, dim):
    pieces = jnp.moveaxis(pieces, 0, dim)
    shape = pieces.shape
    return pieces.reshape(*shape[:dim], shape[dim] * shape[dim + 1], *shape[dim + 2 :])


def gather_directly(array, axis, dim):
    pieces = copy_for_each(array, axis)
    return laid_out(pieces, dim)


def cut_along(array, dim, size):
    before, after = (array.shape[:dim], array.shape[dim + 1 :])
    return jnp.moveaxis(array.reshape(*before, size, -1, *after), dim, 0)


def summed_on_arrival(array, axis, dim):
    size = lax.axis_size(axis)
    pieces = lax.all_to_all(cut_along(array, dim, size), axis, 0, 0, tiled=True)
    return jnp.sum(pieces.astype(jnp.float32), axis=0)


def standardize_features(homolog_embedding):
    mapped_halves = homolog_embedding.astype(jnp.float32)
    center = jnp.mean(mapped_halves, axis=-1, keepdims=True)
    spread = jnp.mean((mapped_halves - center) * (mapped_halves - center), axis=-1, keepdims=True)
    reciprocal_spread = lax.rsqrt(spread + 1e-05)
    return ((mapped_halves - center) * reciprocal_spread, reciprocal_spread)


def regroup(mapped_halves, outer_count, inner_count):
    shaped = mapped_halves.reshape((outer_count, inner_count, -1) + mapped_halves.shape[1:])
    return jnp.swapaxes(shaped, 0, 1).reshape(mapped_halves.shape)


def on_device(
    homolog_embedding,
    split_mapping_matrix,
    couple_mapping_matrix,
    couple_offset_vector,
    incoming_adjoint_couple,
):
    rows_count = lax.axis_size("row")
    cols_count = lax.axis_size("col")
    width = split_mapping_matrix.shape[1] // 2
    standardized_activations, reciprocal_spread = standardize_features(homolog_embedding)
    normalized_input = standardized_activations.astype(jnp.bfloat16)
    factors = jnp.dot(
        normalized_input, split_mapping_matrix, preferred_element_type=jnp.float32
    ).astype(jnp.bfloat16)
    left = factors[..., :width]
    right = factors[..., width:]
    left_part = lax.all_to_all(left, "row", split_axis=1, concat_axis=0, tiled=True)
    left_panel = regroup(gather_directly(left_part, "col", 0), cols_count, rows_count)
    right_part = lax.all_to_all(right, "col", split_axis=1, concat_axis=0, tiled=True)
    right_panel = gather_directly(right_part, "row", 0)
    seq_total = left_panel.shape[0]
    rows_local = left_panel.shape[1]
    cols_local = right_panel.shape[1]
    channels = incoming_adjoint_couple.shape[2]
    step_rows = math.gcd(rows_local, 16)
    count = rows_local // step_rows
    left_blocks = left_panel.reshape(seq_total, count, step_rows, width).transpose(1, 0, 2, 3)
    cot_blocks = incoming_adjoint_couple.reshape(count, step_rows, cols_local, channels)
    bias_wide = couple_offset_vector.astype(jnp.float32)
    weight_back = couple_mapping_matrix.T

    def advance(carry, inputs):
        weight_sum, right_sum = carry
        left_block, cot_block = inputs
        outer = (
            jnp.einsum("sic,sje->ijce", left_block, right_panel, preferred_element_type=jnp.float32)
            / seq_total
        )
        flat = outer.astype(jnp.bfloat16).reshape(step_rows * cols_local, width * width)
        update = (
            jnp.dot(flat, couple_mapping_matrix, preferred_element_type=jnp.float32) + bias_wide
        ).astype(jnp.bfloat16)
        grad_rows = cot_block.reshape(step_rows * cols_local, channels)
        outer_grad = jnp.dot(grad_rows, weight_back, preferred_element_type=jnp.float32).astype(
            jnp.bfloat16
        )
        outer_grad = outer_grad.reshape(step_rows, cols_local, width, width)
        weight_sum = weight_sum + lax.dot_general(
            flat, grad_rows, (((0,), (0,)), ((), ())), preferred_element_type=jnp.float32
        )
        left_grad = (
            jnp.einsum("ijce,sje->sic", outer_grad, right_panel, preferred_element_type=jnp.float32)
            / seq_total
        )
        right_sum = (
            right_sum
            + jnp.einsum(
                "ijce,sic->sje", outer_grad, left_block, preferred_element_type=jnp.float32
            )
            / seq_total
        )
        return (
            (weight_sum, right_sum),
            (update.reshape(step_rows, cols_local, channels), left_grad),
        )

    start = (
        jnp.zeros((width * width, channels), jnp.float32),
        jnp.zeros((seq_total, cols_local, width), jnp.float32),
    )
    (weight_part, right_grad), (updates, left_grads) = lax.scan(
        advance, start, (left_blocks, cot_blocks)
    )
    pair_delta_output = updates.reshape(rows_local, cols_local, channels)
    left_grad = left_grads.transpose(1, 0, 2, 3).reshape(seq_total, rows_local, width)
    left_summed = summed_on_arrival(
        regroup(left_grad, rows_count, cols_count).astype(jnp.bfloat16), "col", 0
    ).astype(jnp.bfloat16)
    left_back = lax.all_to_all(left_summed, "row", split_axis=0, concat_axis=1, tiled=True)
    right_summed = summed_on_arrival(right_grad.astype(jnp.bfloat16), "row", 0).astype(jnp.bfloat16)
    right_back = lax.all_to_all(right_summed, "col", split_axis=0, concat_axis=1, tiled=True)
    factor_weight_gradient = lax.psum(weight_part, ("row", "col"))
    both = jnp.concatenate([left_back, right_back], axis=-1)
    normalized_gradient = jnp.dot(both, split_mapping_matrix.T, preferred_element_type=jnp.float32)
    first_factor = jnp.mean(normalized_gradient, axis=-1, keepdims=True)
    second_factor = jnp.mean(normalized_gradient * standardized_activations, axis=-1, keepdims=True)
    alignment_gradient = (
        reciprocal_spread
        * (normalized_gradient - first_factor - standardized_activations * second_factor)
    ).astype(jnp.bfloat16)
    return (pair_delta_output, alignment_gradient, factor_weight_gradient)


def solution(mesh):
    placed = (P(("row", "col"), None, None), P(), P(), P(), P("row", "col", None))
    return jax.shard_map(
        on_device,
        mesh=mesh,
        in_specs=placed,
        out_specs=(P("row", "col", None), P(("row", "col"), None, None), P()),
        check_vma=False,
    )
```

profile of v0, /device:TPU:1, one launch (start us, length us, event | category | flops | bytes accessed | tf_op | source)
XLA Modules:
  0.0 425.5 jit_solution(13450894267339800620)
XLA Ops:
  11.2 2.3 reduce.7
  14.4 9.3 %all-to-all-start = ((bf16[16,2,1024]{2,1,0:T(2,128)(2,1)}), bf16[16,2,1024]{2,1,0:T(2,128)(2,1)S(1)}, u32[]{:S(2)}, u32[]{:S(2)}) async-start(bf16[16,2,1024]{2,1,0:T(2,128)(2,1)} %reshape.113), calls=%async_computation | async-start | bytes 131072 | tf_op jit(solution)/shard_map/all_to_all | solution.py:67
  24.0 2.3 reduce.8
  27.2 3.8 all-to-all-done
  31.0 4.5 %all-to-all-start.2 = ((bf16[8,2,2048]{2,1,0:T(2,128)(2,1)}), bf16[8,2,2048]{2,1,0:T(2,128)(2,1)S(1)}, u32[]{:S(2)}, u32[]{:S(2)}) async-start(bf16[8,2,2048]{2,1,0:T(2,128)(2,1)} %reshape.117), calls=%async_computation.2 | async-start | bytes 131072 | tf_op jit(solution)/shard_map/all_to_all | solution.py:69
  36.5 1.5 reshape.115
  38.0 2.6 all-to-all-done.2
  40.6 3.5 all-to-all-start.1
  44.8 7.0 %all-to-all-done.1 = bf16[8,2,16384]{2,1,0:T(2,128)(2,1)S(1)} async-done(((bf16[8,2,16384]{2,1,0:T(2,128)(2,1)}), bf16[8,2,16384]{2,1,0:T(2,128)(2,1)S(1)}, u32[]{:S(2)}, u32[]{:S(2)}) %all-to-all-start.1) | async-done | bytes 524320 | tf_op jit(solution)/shard_map/all_to_all | solution.py:10
  53.0 6.9 %all-to-all-start.3 = ((bf16[16,8,128,32]{2,1,3,0:T(8,128)(2,1)}), bf16[16,8,128,32]{2,1,3,0:T(8,128)(2,1)}, u32[]{:S(2)}, u32[]{:S(2)}) async-start(bf16[16,8,128,32]{2,1,3,0:T(8,128)(2,1)} %broadcast_in_dim.48), calls=%async_computation.3 | async-start | bytes 2097152 | tf_op jit(solution)/shard_map/all_to_all | solution.py:10
  60.0 1.6 reshape.116
  63.0 1.9 copy.40
  64.9 3.9 copy.45
  68.8 8.3 %all-to-all-done.3 = bf16[16,8,128,32]{2,1,3,0:T(8,128)(2,1)} async-done(((bf16[16,8,128,32]{2,1,3,0:T(8,128)(2,1)}), bf16[16,8,128,32]{2,1,3,0:T(8,128)(2,1)}, u32[]{:S(2)}, u32[]{:S(2)}) %all-to-all-start.3) | async-done | bytes 1048608 | tf_op jit(solution)/shard_map/all_to_all | solution.py:10
  78.9 128.3 %while.17 = (s32[]{:T(128)}, f32[1024,128]{1,0:T(8,128)}, f32[128,128,32]{1,0,2:T(8,128)S(1)}, bf16[4,16,128,128]{3,2,1,0:T(8,128)(2,1)}, bf16[4,128,16,32]{1,2,...) while((s32[]{:T(128)}, f32[1024,128]{1,0:T(8,128)}, ...), condition=%wide.region_3.4_spmd.clone, body=%wide.region_2.3_spmd.clone.sunk | while | flops 3229941760 | bytes 96995688 | solution.py:121
  79.1 2.3 fusion.88
  81.4 2.7 copy.91
  84.2 2.0 fusion.89
  86.2 1.9 constant_dynamic-update-slice_fusion.2
  88.1 3.5 fusion.90
  91.6 3.2 convolution_convert_fusion.3
  94.8 6.5 %copy.92 = bf16[2048,1024]{0,1:T(8,128)(2,1)} copy(bf16[2048,1024]{1,0:T(8,128)(2,1)} %convolution_convert_fusion.3) | data formatting | bytes 8388608 | tf_op jit(solution)/shard_map/while/body/eval_jaxpr/convert_element_type | solution.py:94
  101.3 3.6 copy.93
  104.9 4.1 fusion.91
  111.2 2.3 fusion.88
  113.4 2.7 copy.91
  116.2 2.0 fusion.89
  118.2 1.9 constant_dynamic-update-slice_fusion.2
  120.1 3.5 fusion.90
  123.6 3.2 convolution_convert_fusion.3
  126.8 6.5 %copy.92 = bf16[2048,1024]{0,1:T(8,128)(2,1)} copy(bf16[2048,1024]{1,0:T(8,128)(2,1)} %convolution_convert_fusion.3) | data formatting | bytes 8388608 | tf_op jit(solution)/shard_map/while/body/eval_jaxpr/convert_element_type | solution.py:94
  133.3 3.6 copy.93
  136.9 4.1 fusion.91
  143.2 2.3 fusion.88
  145.5 2.7 copy.91
  148.2 2.0 fusion.89
  150.2 1.9 constant_dynamic-update-slice_fusion.2
  152.1 3.5 fusion.90
  155.6 3.2 convolution_convert_fusion.3
  158.8 6.5 %copy.92 = bf16[2048,1024]{0,1:T(8,128)(2,1)} copy(bf16[2048,1024]{1,0:T(8,128)(2,1)} %convolution_convert_fusion.3) | data formatting | bytes 8388608 | tf_op jit(solution)/shard_map/while/body/eval_jaxpr/convert_element_type | solution.py:94
  165.4 3.6 copy.93
  169.0 4.1 fusion.91
  175.2 2.3 fusion.88
  177.5 2.7 copy.91
  180.2 2.0 fusion.89
  182.2 1.9 constant_dynamic-update-slice_fusion.2
  184.1 3.5 fusion.90
  187.7 3.2 convolution_convert_fusion.3
  190.8 6.5 %copy.92 = bf16[2048,1024]{0,1:T(8,128)(2,1)} copy(bf16[2048,1024]{1,0:T(8,128)(2,1)} %convolution_convert_fusion.3) | data formatting | bytes 8388608 | tf_op jit(solution)/shard_map/while/body/eval_jaxpr/convert_element_type | solution.py:94
  197.4 3.6 copy.93
  201.0 4.1 fusion.91
  207.2 5.3 %copy.47 = bf16[128,4,16,32]{3,2,1,0:T(8,128)(2,1)} copy(bf16[128,4,16,32]{0,2,3,1:T(8,128)(2,1)} %bitcast.181) | data formatting | bytes 1048576 | tf_op jit(solution)/shard_map/convert_element_type | solution.py:127
  212.5 2.0 copy.48
  214.5 1.5 reshape.119
  216.1 3.5 all-to-all-start.4
  222.2 6.0 %all-to-all-done.4 = bf16[8,2,16384]{2,1,0:T(2,128)(2,1)S(1)} async-done(((bf16[8,2,16384]{2,1,0:T(2,128)(2,1)}), bf16[8,2,16384]{2,1,0:T(2,128)(2,1)S(1)}, u32[]{:S(2)}, u32[]{:S(2)}) %all-to-all-start.4) | async-done | bytes 524320 | tf_op jit(solution)/shard_map/all_to_all | solution.py:33
  228.2 5.7 %all-to-all-start.6 = ((bf16[16,8,128,32]{2,1,3,0:T(8,128)(2,1)}), bf16[16,8,128,32]{2,1,3,0:T(8,128)(2,1)S(1)}, u32[]{:S(2)}, u32[]{:S(2)}) async-start(bf16[16,8,128,32]{2,1,3,0:T(8,128)(2,1)} %copy.51), calls=%async_computation.6 | async-start | bytes 2097152 | tf_op jit(solution)/shard_map/all_to_all | solution.py:33
  235.6 15.3 %all-to-all-done.6 = bf16[16,8,128,32]{2,1,3,0:T(8,128)(2,1)S(1)} async-done(((bf16[16,8,128,32]{2,1,3,0:T(8,128)(2,1)}), bf16[16,8,128,32]{2,1,3,0:T(8,128)(2,1)S(1)}, u32[]{:S(2)}, u32[]{:S(2)}) %all-to-all-start.6) | async-done | bytes 1048608 | tf_op jit(solution)/shard_map/all_to_all | solution.py:33
  250.9 4.4 %all-to-all-start.5 = ((bf16[16,2,1024]{2,1,0:T(2,128)(2,1)}), bf16[16,2,1024]{2,1,0:T(2,128)(2,1)S(1)}, u32[]{:S(2)}, u32[]{:S(2)}) async-start(bf16[16,2,1024]{2,1,0:T(2,128)(2,1)} %reshape.121), calls=%async_computation.5 | async-start | bytes 131072 | tf_op jit(solution)/shard_map/all_to_all | solution.py:129
  256.0 6.6 %all-to-all-done.5 = bf16[16,2,1024]{2,1,0:T(2,128)(2,1)S(1)} async-done(((bf16[16,2,1024]{2,1,0:T(2,128)(2,1)}), bf16[16,2,1024]{2,1,0:T(2,128)(2,1)S(1)}, u32[]{:S(2)}, u32[]{:S(2)}) %all-to-all-start.5) | async-done | bytes 65568 | tf_op jit(solution)/shard_map/all_to_all | solution.py:129
  262.7 3.4 all-to-all-start.7
  267.1 3.9 all-to-all-done.7
  272.1 144.7 %all-reduce.2.cloned.1.call-done = f32[1024,128]{1,0:T(8,128)} async-done(((f32[1024,128]{1,0:T(8,128)}), f32[1024,128]{1,0:T(8,128)}) %all-reduce.2.cloned.1.call-update) | async-done | bytes 524304 | tf_op jit(solution)/shard_map/psum | solution.py:132
  416.8 1.9 copy.112
  (123 shorter events, 28.0 us)
Async XLA Ops:
  7.2 1.9 copy-start
  14.4 16.7 %all-to-all-start = ((bf16[16,2,1024]{2,1,0:T(2,128)(2,1)}), bf16[16,2,1024]{2,1,0:T(2,128)(2,1)S(1)}, u32[]{:S(2)}, u32[]{:S(2)}) async-start(bf16[16,2,1024]{2,1,0:T(2,128)(2,1)} %reshape.113), calls=%async_computation | async-start | bytes 131072 | tf_op jit(solution)/shard_map/all_to_all | solution.py:67
  31.0 9.6 %all-to-all-start.2 = ((bf16[8,2,2048]{2,1,0:T(2,128)(2,1)}), bf16[8,2,2048]{2,1,0:T(2,128)(2,1)S(1)}, u32[]{:S(2)}, u32[]{:S(2)}) async-start(bf16[8,2,2048]{2,1,0:T(2,128)(2,1)} %reshape.117), calls=%async_computation.2 | async-start | bytes 131072 | tf_op jit(solution)/shard_map/all_to_all | solution.py:69
  36.3 23.5 %copy-start.9 = (bf16[1024,128]{1,0:T(8,128)(2,1)S(1)}, bf16[1024,128]{1,0:T(8,128)(2,1)}, u32[]{:S(2)}) copy-start(bf16[1024,128]{1,0:T(8,128)(2,1)} %param.9) | copy-start | bytes 786436
  36.3 23.7 %copy-start.11 = (bf16[128]{0:T(256)(128)(2,1)S(1)}, bf16[128]{0:T(256)(128)(2,1)}, u32[]{:S(2)}) copy-start(bf16[128]{0:T(256)(128)(2,1)} %param.10) | copy-start | bytes 772
  40.6 11.2 %all-to-all-start.1 = ((bf16[8,2,16384]{2,1,0:T(2,128)(2,1)}), bf16[8,2,16384]{2,1,0:T(2,128)(2,1)S(1)}, u32[]{:S(2)}, u32[]{:S(2)}) async-start(bf16[8,2,16384]{2,1,0:T(2,128)(2,1)} %reshape.115), calls=%async_computation.1 | async-start | bytes 1048576 | tf_op jit(solution)/shard_map/all_to_all | solution.py:10
  53.0 24.0 %all-to-all-start.3 = ((bf16[16,8,128,32]{2,1,3,0:T(8,128)(2,1)}), bf16[16,8,128,32]{2,1,3,0:T(8,128)(2,1)}, u32[]{:S(2)}, u32[]{:S(2)}) async-start(bf16[16,8,128,32]{2,1,3,0:T(8,128)(2,1)} %broadcast_in_dim.48), calls=%async_computation.3 | async-start | bytes 2097152 | tf_op jit(solution)/shard_map/all_to_all | solution.py:10
  79.1 5.1 %copy-start.2 = (bf16[128,128,32]{1,0,2:T(8,128)(2,1)}, bf16[128,128,32]{1,0,2:T(8,128)(2,1)S(1)}, u32[]{:S(2)}) copy-start(bf16[128,128,32]{1,0,2:T(8,128)(2,1)S(1)} %get-tuple-element.269) | copy-start | bytes 3145732 | tf_op jit(solution)/shard_map/while
  81.4 2.7 copy-start.10
  84.1 4.0 copy-start.1
  84.2 3.9 copy-start.7
  91.6 3.2 copy-start.8
  104.9 4.1 copy-start.3
  104.9 4.1 copy-start.5
  110.4 0.8 copy-start.6
  111.2 5.0 %copy-start.2 = (bf16[128,128,32]{1,0,2:T(8,128)(2,1)}, bf16[128,128,32]{1,0,2:T(8,128)(2,1)S(1)}, u32[]{:S(2)}) copy-start(bf16[128,128,32]{1,0,2:T(8,128)(2,1)S(1)} %get-tuple-element.269) | copy-start | bytes 3145732 | tf_op jit(solution)/shard_map/while
  113.4 2.7 copy-start.10
  116.2 4.0 copy-start.1
  116.2 3.9 copy-start.7
  123.6 3.2 copy-start.8
  136.9 4.1 copy-start.3
  136.9 4.1 copy-start.5
  142.4 0.8 copy-start.6
  143.2 5.0 %copy-start.2 = (bf16[128,128,32]{1,0,2:T(8,128)(2,1)}, bf16[128,128,32]{1,0,2:T(8,128)(2,1)S(1)}, u32[]{:S(2)}) copy-start(bf16[128,128,32]{1,0,2:T(8,128)(2,1)S(1)} %get-tuple-element.269) | copy-start | bytes 3145732 | tf_op jit(solution)/shard_map/while
  145.4 2.7 copy-start.10
  148.2 4.0 copy-start.1
  148.2 3.9 copy-start.7
  155.6 3.2 copy-start.8
  168.9 4.1 copy-start.3
  169.0 4.1 copy-start.5
  174.4 0.8 copy-start.6
  175.2 5.0 %copy-start.2 = (bf16[128,128,32]{1,0,2:T(8,128)(2,1)}, bf16[128,128,32]{1,0,2:T(8,128)(2,1)S(1)}, u32[]{:S(2)}) copy-start(bf16[128,128,32]{1,0,2:T(8,128)(2,1)S(1)} %get-tuple-element.269) | copy-start | bytes 3145732 | tf_op jit(solution)/shard_map/while
  177.5 2.7 copy-start.10
  180.2 4.0 copy-start.1
  180.2 3.9 copy-start.7
  187.6 3.2 copy-start.8
  201.0 4.1 copy-start.3
  201.0 4.1 copy-start.5
  206.4 0.8 copy-start.6
  216.1 12.1 %all-to-all-start.4 = ((bf16[8,2,16384]{2,1,0:T(2,128)(2,1)}), bf16[8,2,16384]{2,1,0:T(2,128)(2,1)S(1)}, u32[]{:S(2)}, u32[]{:S(2)}) async-start(bf16[8,2,16384]{2,1,0:T(2,128)(2,1)} %reshape.119), calls=%async_computation.4 | async-start | bytes 1048576 | tf_op jit(solution)/shard_map/all_to_all | solution.py:33
  222.2 48.9 %copy-start.4 = (bf16[1,1024,64]{1,2,0:T(8,128)(2,1)S(1)}, bf16[1,1024,64]{1,2,0:T(8,128)(2,1)}, u32[]{:S(2)}) copy-start(bf16[1,1024,64]{1,2,0:T(8,128)(2,1)} %param.7) | copy-start | bytes 393220
  228.2 22.7 %all-to-all-start.6 = ((bf16[16,8,128,32]{2,1,3,0:T(8,128)(2,1)}), bf16[16,8,128,32]{2,1,3,0:T(8,128)(2,1)S(1)}, u32[]{:S(2)}, u32[]{:S(2)}) async-start(bf16[16,8,128,32]{2,1,3,0:T(8,128)(2,1)} %copy.51), calls=%async_computation.6 | async-start | bytes 2097152 | tf_op jit(solution)/shard_map/all_to_all | solution.py:33
  250.9 11.8 %all-to-all-start.5 = ((bf16[16,2,1024]{2,1,0:T(2,128)(2,1)}), bf16[16,2,1024]{2,1,0:T(2,128)(2,1)S(1)}, u32[]{:S(2)}, u32[]{:S(2)}) async-start(bf16[16,2,1024]{2,1,0:T(2,128)(2,1)} %reshape.121), calls=%async_computation.5 | async-start | bytes 131072 | tf_op jit(solution)/shard_map/all_to_all | solution.py:129
  262.7 8.4 %all-to-all-start.7 = ((bf16[8,128,32]{1,2,0:T(8,128)(2,1)}), bf16[8,128,32]{1,2,0:T(8,128)(2,1)S(1)}, u32[]{:S(2)}, u32[]{:S(2)}) async-start(bf16[8,128,32]{1,2,0:T(8,128)(2,1)} %copy.53), calls=%async_computation.7 | async-start | bytes 131072 | tf_op jit(solution)/shard_map/all_to_all | solution.py:131
  266.0 150.8 %all-reduce.2.cloned.1.call-start = ((), (), s32[]{:S(2)}) async-start(), calls=%async_computation.8 | async-start | bytes 1048576 | tf_op jit(solution)/shard_map/psum | solution.py:132
Sparse Core Ops, SparseCore 0:
  272.2 144.5 all-reduce.1
where the time goes:
time: 428 us; the launch traced here: 426 us
  waiting for transfers between devices  199 us (46%)
  local copies, waits for them, and re-layouts  96.1 us (22%)
  matrix products  66.7 us (16%)
  starting transfers between devices  41.1 us (10%)
  between operations  14.4 us (3%)
  other arithmetic  7.57 us (2%)
    psum x1, waiting for transfers between devices, on_device(): factor_weight_gradient = lax.psum(weight_part, ('row', 'col'))  145 us
    convert_element_type x4, local copies, waits for them, and re-layouts, advance(): jnp.dot(grad_rows, weight_back, preferred_element_type=jnp.float32)  26.1 us
    all_to_all x2, waiting for transfers between devices, summed_on_arrival(): pieces = lax.all_to_all(cut_along(array, dim, size), axis, 0, 0, tiled=True)  21.3 us
    while x68, local copies, waits for them, and re-layouts  17.6 us
    dot_general x4, matrix products, advance(): jnp.einsum('ijce,sic->sje', outer_grad, left_block, preferred_element_typ...  16.3 us
    unnamed x25, local copies, waits for them, and re-layouts  15.8 us
    all_to_all x2, waiting for transfers between devices, copy_for_each(): lax.all_to_all(jnp.broadcast_to(array[None], (size, *array.shape)), axis,...  15.2 us
    dot_general x4, matrix products, advance(): lax.dot_general(flat, grad_rows, (((0,), (0,)), ((), ())), preferred_elem...  14 us
  transfers between devices with their start and end apart: 9, of which 9 were waited for; matrix products, arithmetic and copies ran while one was open for 5% of the time, Pallas kernels for 0%

commit v1 on v0

--- a/solution.py
+++ b/solution.py
@@ -129,7 +129,7 @@
     left_back = lax.all_to_all(left_summed, "row", split_axis=0, concat_axis=1, tiled=True)
     right_summed = summed_on_arrival(right_grad.astype(jnp.bfloat16), "row", 0).astype(jnp.bfloat16)
     right_back = lax.all_to_all(right_summed, "col", split_axis=0, concat_axis=1, tiled=True)
-    factor_weight_gradient = lax.psum(weight_part, ("row", "col"))
+    factor_weight_gradient = lax.psum(lax.psum(weight_part, "row"), "col")
     both = jnp.concatenate([left_back, right_back], axis=-1)
     normalized_gradient = jnp.dot(both, split_mapping_matrix.T, preferred_element_type=jnp.float32)
     first_factor = jnp.mean(normalized_gradient, axis=-1, keepdims=True)

time: 428 us -> 466 us (1.089)
  waiting for transfers between devices: 199 us -> 232 us
    psum x1 -> x2, waiting for transfers between devices: 145 us -> 183 us  [on_device(): factor_weight_gradient = lax.psum(lax.psum(weight_part, 'row'), 'col')]
  transfers between devices with their start and end apart: 9 -> 10, of which waited for: 9 -> 9; matrix products, arithmetic and copies ran while one was open for 5% -> 5% of each run, Pallas kernels for 0% -> 0%
where the time goes in v1:
time: 466 us; the launch traced here: 459 us
  waiting for transfers between devices  232 us (50%)
  local copies, waits for them, and re-layouts  96.1 us (21%)
  matrix products  66.7 us (14%)
  starting transfers between devices  41.2 us (9%)
  between operations  14.4 us (3%)
  other arithmetic  7.57 us (2%)
    psum x2, waiting for transfers between devices, on_device(): factor_weight_gradient = lax.psum(lax.psum(weight_part, 'row'), 'col')  183 us
    convert_element_type x4, local copies, waits for them, and re-layouts, advance(): jnp.dot(grad_rows, weight_back, preferred_element_type=jnp.float32)  26.1 us
    all_to_all x2, waiting for transfers between devices, summed_on_arrival(): pieces = lax.all_to_all(cut_along(array, dim, size), axis, 0, 0, tiled=True)  20.6 us
    while x68, local copies, waits for them, and re-layouts  17.6 us
    dot_general x4, matrix products, advance(): jnp.einsum('ijce,sic->sje', outer_grad, left_block, preferred_element_typ...  16.3 us
    unnamed x25, local copies, waits for them, and re-layouts  15.8 us
    all_to_all x2, waiting for transfers between devices, copy_for_each(): lax.all_to_all(jnp.broadcast_to(array[None], (size, *array.shape)), axis,...  15.2 us
    dot_general x4, matrix products, advance(): lax.dot_general(flat, grad_rows, (((0,), (0,)), ((), ())), preferred_elem...  14 us
  transfers between devices with their start and end apart: 10, of which 9 were waited for; matrix products, arithmetic and copies ran while one was open for 5% of the time, Pallas kernels for 0%

profile of v1, /device:TPU:1, one launch (start us, length us, event | category | flops | bytes accessed | tf_op | source)
XLA Modules:
  0.0 459.0 jit_solution(9826051068119240061)
XLA Ops:
  11.2 2.3 reduce.7
  14.4 9.3 %all-to-all-start = ((bf16[16,2,1024]{2,1,0:T(2,128)(2,1)}), bf16[16,2,1024]{2,1,0:T(2,128)(2,1)S(1)}, u32[]{:S(2)}, u32[]{:S(2)}) async-start(bf16[16,2,1024]{2,1,0:T(2,128)(2,1)} %reshape.113), calls=%async_computation | async-start | bytes 131072 | tf_op jit(solution)/shard_map/all_to_all | solution.py:67
  24.0 2.3 reduce.8
  27.2 3.8 all-to-all-done
  31.0 4.5 all-to-all-start.2
  36.5 1.5 reshape.115
  38.0 2.6 all-to-all-done.2
  40.6 3.5 all-to-all-start.1
  44.8 7.0 %all-to-all-done.1 = bf16[8,2,16384]{2,1,0:T(2,128)(2,1)S(1)} async-done(((bf16[8,2,16384]{2,1,0:T(2,128)(2,1)}), bf16[8,2,16384]{2,1,0:T(2,128)(2,1)S(1)}, u32[]{:S(2)}, u32[]{:S(2)}) %all-to-all-start.1) | async-done | bytes 524320 | tf_op jit(solution)/shard_map/all_to_all | solution.py:10
  53.0 6.9 %all-to-all-start.3 = ((bf16[16,8,128,32]{2,1,3,0:T(8,128)(2,1)}), bf16[16,8,128,32]{2,1,3,0:T(8,128)(2,1)}, u32[]{:S(2)}, u32[]{:S(2)}) async-start(bf16[16,8,128,32]{2,1,3,0:T(8,128)(2,1)} %broadcast_in_dim.48), calls=%async_computation.3 | async-start | bytes 2097152 | tf_op jit(solution)/shard_map/all_to_all | solution.py:10
  60.0 1.6 reshape.116
  63.0 1.9 copy.40
  64.9 3.9 copy.45
  68.8 8.3 %all-to-all-done.3 = bf16[16,8,128,32]{2,1,3,0:T(8,128)(2,1)} async-done(((bf16[16,8,128,32]{2,1,3,0:T(8,128)(2,1)}), bf16[16,8,128,32]{2,1,3,0:T(8,128)(2,1)}, u32[]{:S(2)}, u32[]{:S(2)}) %all-to-all-start.3) | async-done | bytes 1048608 | tf_op jit(solution)/shard_map/all_to_all | solution.py:10
  78.9 128.3 %while.17 = (s32[]{:T(128)}, f32[1024,128]{1,0:T(8,128)}, f32[128,128,32]{1,0,2:T(8,128)S(1)}, bf16[4,16,128,128]{3,2,1,0:T(8,128)(2,1)}, bf16[4,128,16,32]{1,2,...) while((s32[]{:T(128)}, f32[1024,128]{1,0:T(8,128)}, ...), condition=%wide.region_3.4_spmd.clone, body=%wide.region_2.3_spmd.clone.sunk | while | flops 3229941760 | bytes 96995688 | solution.py:121
  79.1 2.3 fusion.88
  81.4 2.7 copy.91
  84.2 2.0 fusion.89
  86.2 1.9 constant_dynamic-update-slice_fusion.2
  88.1 3.5 fusion.90
  91.6 3.2 convolution_convert_fusion.3
  94.8 6.5 %copy.92 = bf16[2048,1024]{0,1:T(8,128)(2,1)} copy(bf16[2048,1024]{1,0:T(8,128)(2,1)} %convolution_convert_fusion.3) | data formatting | bytes 8388608 | tf_op jit(solution)/shard_map/while/body/eval_jaxpr/convert_element_type | solution.py:94
  101.3 3.6 copy.93
  104.9 4.1 fusion.91
  111.2 2.3 fusion.88
  113.4 2.7 copy.91
  116.2 2.0 fusion.89
  118.2 1.9 constant_dynamic-update-slice_fusion.2
  120.1 3.5 fusion.90
  123.6 3.2 convolution_convert_fusion.3
  126.8 6.5 %copy.92 = bf16[2048,1024]{0,1:T(8,128)(2,1)} copy(bf16[2048,1024]{1,0:T(8,128)(2,1)} %convolution_convert_fusion.3) | data formatting | bytes 8388608 | tf_op jit(solution)/shard_map/while/body/eval_jaxpr/convert_element_type | solution.py:94
  133.3 3.6 copy.93
  136.9 4.1 fusion.91
  143.2 2.3 fusion.88
  145.5 2.7 copy.91
  148.2 2.0 fusion.89
  150.2 1.9 constant_dynamic-update-slice_fusion.2
  152.1 3.5 fusion.90
  155.6 3.2 convolution_convert_fusion.3
  158.8 6.5 %copy.92 = bf16[2048,1024]{0,1:T(8,128)(2,1)} copy(bf16[2048,1024]{1,0:T(8,128)(2,1)} %convolution_convert_fusion.3) | data formatting | bytes 8388608 | tf_op jit(solution)/shard_map/while/body/eval_jaxpr/convert_element_type | solution.py:94
  165.4 3.6 copy.93
  169.0 4.1 fusion.91
  175.2 2.3 fusion.88
  177.5 2.7 copy.91
  180.2 2.0 fusion.89
  182.2 1.9 constant_dynamic-update-slice_fusion.2
  184.1 3.5 fusion.90
  187.7 3.2 convolution_convert_fusion.3
  190.8 6.5 %copy.92 = bf16[2048,1024]{0,1:T(8,128)(2,1)} copy(bf16[2048,1024]{1,0:T(8,128)(2,1)} %convolution_convert_fusion.3) | data formatting | bytes 8388608 | tf_op jit(solution)/shard_map/while/body/eval_jaxpr/convert_element_type | solution.py:94
  197.4 3.6 copy.93
  201.0 4.1 fusion.91
  207.2 5.3 %copy.47 = bf16[128,4,16,32]{3,2,1,0:T(8,128)(2,1)} copy(bf16[128,4,16,32]{0,2,3,1:T(8,128)(2,1)} %bitcast.181) | data formatting | bytes 1048576 | tf_op jit(solution)/shard_map/convert_element_type | solution.py:127
  212.5 2.0 copy.48
  214.5 1.5 reshape.119
  216.1 3.5 all-to-all-start.4
  222.2 6.0 %all-to-all-done.4 = bf16[8,2,16384]{2,1,0:T(2,128)(2,1)S(1)} async-done(((bf16[8,2,16384]{2,1,0:T(2,128)(2,1)}), bf16[8,2,16384]{2,1,0:T(2,128)(2,1)S(1)}, u32[]{:S(2)}, u32[]{:S(2)}) %all-to-all-start.4) | async-done | bytes 524320 | tf_op jit(solution)/shard_map/all_to_all | solution.py:33
  228.2 5.7 %all-to-all-start.6 = ((bf16[16,8,128,32]{2,1,3,0:T(8,128)(2,1)}), bf16[16,8,128,32]{2,1,3,0:T(8,128)(2,1)S(1)}, u32[]{:S(2)}, u32[]{:S(2)}) async-start(bf16[16,8,128,32]{2,1,3,0:T(8,128)(2,1)} %copy.51), calls=%async_computation.6 | async-start | bytes 2097152 | tf_op jit(solution)/shard_map/all_to_all | solution.py:33
  236.3 14.6 %all-to-all-done.6 = bf16[16,8,128,32]{2,1,3,0:T(8,128)(2,1)S(1)} async-done(((bf16[16,8,128,32]{2,1,3,0:T(8,128)(2,1)}), bf16[16,8,128,32]{2,1,3,0:T(8,128)(2,1)S(1)}, u32[]{:S(2)}, u32[]{:S(2)}) %all-to-all-start.6) | async-done | bytes 1048608 | tf_op jit(solution)/shard_map/all_to_all | solution.py:33
  250.9 4.4 all-to-all-start.5
  256.1 6.7 %all-to-all-done.5 = bf16[16,2,1024]{2,1,0:T(2,128)(2,1)S(1)} async-done(((bf16[16,2,1024]{2,1,0:T(2,128)(2,1)}), bf16[16,2,1024]{2,1,0:T(2,128)(2,1)S(1)}, u32[]{:S(2)}, u32[]{:S(2)}) %all-to-all-start.5) | async-done | bytes 65568 | tf_op jit(solution)/shard_map/all_to_all | solution.py:129
  262.7 3.4 all-to-all-start.7
  266.5 110.5 %all-reduce.3.cloned.1.call-done = f32[1024,128]{1,0:T(8,128)} async-done(((f32[1024,128]{1,0:T(8,128)}), f32[1024,128]{1,0:T(8,128)}) %all-reduce.3.cloned.1.call-update) | async-done | bytes 524304 | tf_op jit(solution)/shard_map/psum | solution.py:132
  378.1 72.2 %all-reduce.5.cloned.1.call-done = f32[1024,128]{1,0:T(8,128)} async-done(((f32[1024,128]{1,0:T(8,128)}), f32[1024,128]{1,0:T(8,128)}) %all-reduce.5.cloned.1.call-update) | async-done | bytes 524304 | tf_op jit(solution)/shard_map/psum | solution.py:132
  450.2 1.9 copy.113
  (126 shorter events, 28.0 us)
Async XLA Ops:
  7.2 1.9 copy-start
  14.4 16.7 %all-to-all-start = ((bf16[16,2,1024]{2,1,0:T(2,128)(2,1)}), bf16[16,2,1024]{2,1,0:T(2,128)(2,1)S(1)}, u32[]{:S(2)}, u32[]{:S(2)}) async-start(bf16[16,2,1024]{2,1,0:T(2,128)(2,1)} %reshape.113), calls=%async_computation | async-start | bytes 131072 | tf_op jit(solution)/shard_map/all_to_all | solution.py:67
  31.0 9.6 %all-to-all-start.2 = ((bf16[8,2,2048]{2,1,0:T(2,128)(2,1)}), bf16[8,2,2048]{2,1,0:T(2,128)(2,1)S(1)}, u32[]{:S(2)}, u32[]{:S(2)}) async-start(bf16[8,2,2048]{2,1,0:T(2,128)(2,1)} %reshape.117), calls=%async_computation.2 | async-start | bytes 131072 | tf_op jit(solution)/shard_map/all_to_all | solution.py:69
  36.3 23.5 %copy-start.9 = (bf16[1024,128]{1,0:T(8,128)(2,1)S(1)}, bf16[1024,128]{1,0:T(8,128)(2,1)}, u32[]{:S(2)}) copy-start(bf16[1024,128]{1,0:T(8,128)(2,1)} %param.9) | copy-start | bytes 786436
  36.3 23.7 %copy-start.11 = (bf16[128]{0:T(256)(128)(2,1)S(1)}, bf16[128]{0:T(256)(128)(2,1)}, u32[]{:S(2)}) copy-start(bf16[128]{0:T(256)(128)(2,1)} %param.10) | copy-start | bytes 772
  40.6 11.2 %all-to-all-start.1 = ((bf16[8,2,16384]{2,1,0:T(2,128)(2,1)}), bf16[8,2,16384]{2,1,0:T(2,128)(2,1)S(1)}, u32[]{:S(2)}, u32[]{:S(2)}) async-start(bf16[8,2,16384]{2,1,0:T(2,128)(2,1)} %reshape.115), calls=%async_computation.1 | async-start | bytes 1048576 | tf_op jit(solution)/shard_map/all_to_all | solution.py:10
  53.0 24.0 %all-to-all-start.3 = ((bf16[16,8,128,32]{2,1,3,0:T(8,128)(2,1)}), bf16[16,8,128,32]{2,1,3,0:T(8,128)(2,1)}, u32[]{:S(2)}, u32[]{:S(2)}) async-start(bf16[16,8,128,32]{2,1,3,0:T(8,128)(2,1)} %broadcast_in_dim.48), calls=%async_computation.3 | async-start | bytes 2097152 | tf_op jit(solution)/shard_map/all_to_all | solution.py:10
  79.1 5.1 %copy-start.2 = (bf16[128,128,32]{1,0,2:T(8,128)(2,1)}, bf16[128,128,32]{1,0,2:T(8,128)(2,1)S(1)}, u32[]{:S(2)}) copy-start(bf16[128,128,32]{1,0,2:T(8,128)(2,1)S(1)} %get-tuple-element.269) | copy-start | bytes 3145732 | tf_op jit(solution)/shard_map/while
  81.4 2.7 copy-start.10
  84.1 4.0 copy-start.1
  84.2 3.9 copy-start.7
  91.6 3.2 copy-start.8
  104.9 4.1 copy-start.3
  104.9 4.1 copy-start.5
  110.4 0.8 copy-start.6
  111.2 5.0 %copy-start.2 = (bf16[128,128,32]{1,0,2:T(8,128)(2,1)}, bf16[128,128,32]{1,0,2:T(8,128)(2,1)S(1)}, u32[]{:S(2)}) copy-start(bf16[128,128,32]{1,0,2:T(8,128)(2,1)S(1)} %get-tuple-element.269) | copy-start | bytes 3145732 | tf_op jit(solution)/shard_map/while
  113.4 2.7 copy-start.10
  116.2 4.0 copy-start.1
  116.2 3.9 copy-start.7
  123.6 3.2 copy-start.8
  136.9 4.1 copy-start.3
  136.9 4.1 copy-start.5
  142.4 0.8 copy-start.6
  143.2 5.0 %copy-start.2 = (bf16[128,128,32]{1,0,2:T(8,128)(2,1)}, bf16[128,128,32]{1,0,2:T(8,128)(2,1)S(1)}, u32[]{:S(2)}) copy-start(bf16[128,128,32]{1,0,2:T(8,128)(2,1)S(1)} %get-tuple-element.269) | copy-start | bytes 3145732 | tf_op jit(solution)/shard_map/while
  145.4 2.7 copy-start.10
  148.2 4.0 copy-start.1
  148.2 3.9 copy-start.7
  155.6 3.2 copy-start.8
  168.9 4.1 copy-start.3
  169.0 4.1 copy-start.5
  174.4 0.8 copy-start.6
  175.2 5.0 %copy-start.2 = (bf16[128,128,32]{1,0,2:T(8,128)(2,1)}, bf16[128,128,32]{1,0,2:T(8,128)(2,1)S(1)}, u32[]{:S(2)}) copy-start(bf16[128,128,32]{1,0,2:T(8,128)(2,1)S(1)} %get-tuple-element.269) | copy-start | bytes 3145732 | tf_op jit(solution)/shard_map/while
  177.5 2.7 copy-start.10
  180.2 4.0 copy-start.1
  180.2 3.9 copy-start.7
  187.6 3.2 copy-start.8
  201.0 4.1 copy-start.3
  201.0 4.1 copy-start.5
  206.4 0.8 copy-start.6
  216.1 12.1 %all-to-all-start.4 = ((bf16[8,2,16384]{2,1,0:T(2,128)(2,1)}), bf16[8,2,16384]{2,1,0:T(2,128)(2,1)S(1)}, u32[]{:S(2)}, u32[]{:S(2)}) async-start(bf16[8,2,16384]{2,1,0:T(2,128)(2,1)} %reshape.119), calls=%async_computation.4 | async-start | bytes 1048576 | tf_op jit(solution)/shard_map/all_to_all | solution.py:33
  222.2 154.9 %copy-start.4 = (bf16[1,1024,64]{1,2,0:T(8,128)(2,1)S(1)}, bf16[1,1024,64]{1,2,0:T(8,128)(2,1)}, u32[]{:S(2)}) copy-start(bf16[1,1024,64]{1,2,0:T(8,128)(2,1)} %param.7) | copy-start | bytes 393220
  228.2 22.7 %all-to-all-start.6 = ((bf16[16,8,128,32]{2,1,3,0:T(8,128)(2,1)}), bf16[16,8,128,32]{2,1,3,0:T(8,128)(2,1)S(1)}, u32[]{:S(2)}, u32[]{:S(2)}) async-start(bf16[16,8,128,32]{2,1,3,0:T(8,128)(2,1)} %copy.51), calls=%async_computation.6 | async-start | bytes 2097152 | tf_op jit(solution)/shard_map/all_to_all | solution.py:33
  233.9 143.1 %all-reduce.3.cloned.1.call-start = ((), (), s32[]{:S(2)}) async-start(), calls=%async_computation.8 | async-start | bytes 1048576 | tf_op jit(solution)/shard_map/psum | solution.py:132
  250.9 11.8 %all-to-all-start.5 = ((bf16[16,2,1024]{2,1,0:T(2,128)(2,1)}), bf16[16,2,1024]{2,1,0:T(2,128)(2,1)S(1)}, u32[]{:S(2)}, u32[]{:S(2)}) async-start(bf16[16,2,1024]{2,1,0:T(2,128)(2,1)} %reshape.121), calls=%async_computation.5 | async-start | bytes 131072 | tf_op jit(solution)/shard_map/all_to_all | solution.py:129
  262.7 114.3 %all-to-all-start.7 = ((bf16[8,128,32]{1,2,0:T(8,128)(2,1)}), bf16[8,128,32]{1,2,0:T(8,128)(2,1)S(1)}, u32[]{:S(2)}, u32[]{:S(2)}) async-start(bf16[8,128,32]{1,2,0:T(8,128)(2,1)} %copy.53), calls=%async_computation.7 | async-start | bytes 131072 | tf_op jit(solution)/shard_map/all_to_all | solution.py:131
  266.1 184.2 %all-reduce.5.cloned.1.call-start = ((), (), s32[]{:S(2)}) async-start(), calls=%async_computation.9 | async-start | bytes 1048576 | tf_op jit(solution)/shard_map/psum | solution.py:132
Sparse Core Ops, SparseCore 0:
  237.8 139.1 all-reduce.2
  379.5 70.7 all-reduce.4
